TPU v7x, 32 devices: a whole 2x2x4 slice. The times are simulated.
32 devices in a mesh: lat: 8 (over y, x, core), lev: 4 (over z).
Axes of the slice: x: 2, y: 2, z: 4, core: 2. Of those that a mesh axis runs over, the one named last changes fastest.
Arguments:
- fourier: bfloat16 [64, 2560, 128], P('lev', 'lat'), may hold values from -6 to 6
- quad_weights: float32 [2560], P('lat'), may hold values from 0.005 to 0.05
- legendre: bfloat16 [2560, 64, 1280], P('lat'), may hold values from -6 to 6
- owner_pair: int32 [64], replicated, may hold values from 0 to 63, each once
Outputs:
- spectra: float32 [64, 64, 1280], P('lat', 'lev')
- energy: float32 [], replicated
Inputs may be any that keep to these rules, and one draw needn't show every extreme that they name: `owner_pair`: a permutation of 0 to 63.
All inputs are finite; a program needn't handle non-finite values.
Results may differ from a plain program's by a relative error of at most 0.00094.
Values may be sent and summed in bfloat16 or wider, within the bound.
A program may use at most 192 MiB of HBM per device.

v0:
```python
import functools

import jax
import jax.numpy as jnp
from jax import lax
from jax.experimental import pallas as pl
from jax.experimental.pallas import tpu as pltpu
from jax.sharding import PartitionSpec as P

SPACING = 10
GROUP = 8
HALVES = 2
MESH = pl.DeviceIdType.MESH


def remote(src, dst, send, recv, device):
    return pltpu.make_async_remote_copy(
        src_ref=src, dst_ref=dst, send_sem=send, recv_sem=recv, device_id=device, device_id_type=MESH
    )


def kernel(
    cfg,
    owner_ref,
    wave_ref,
    leg_ref,
    out_ref,
    energy_ref,
    lhs,
    part,
    pair_out,
    pair_in,
    chip_out,
    chip_in,
    esum,
    elat,
    elev,
    pair_send,
    pair_recv,
    chip_send,
    chip_recv,
    elat_send,
    elat_recv,
    elev_send,
    elev_recv,
):
    n_lat, n_lev, ch, lats, pairs, length, width, steps, m_win = cfg
    t = pl.program_id(0)
    h = pl.program_id(1)
    lat = lax.axis_index("lat")
    lev = lax.axis_index("lev")
    core = lax.rem(lat, 2)
    chip = lat // 2
    chips = n_lat // 2
    own = pairs // n_lat
    rows = GROUP * ch
    groups = pairs // GROUP
    half_groups = groups // HALVES
    barrier = pltpu.get_barrier_semaphore()

    @pl.when((t == 0) & (h == 0))
    def _():
        for d in range(1, n_lat):
            pl.semaphore_signal(
                barrier, inc=1, device_id=(lax.rem(lat + d, n_lat), lev), device_id_type=MESH
            )
        for d in range(1, n_lev):
            pl.semaphore_signal(
                barrier, inc=1, device_id=(lat, lax.rem(lev + d, n_lev)), device_id_type=MESH
            )
        esum[...] = jnp.zeros_like(esum)

    @pl.when(t == 0)
    def _():
        def build(step, carry):
            g = h * half_groups + step
            for start in range(0, lats * GROUP, 256):
                size = min(256, lats * GROUP - start)
                first = start // GROUP
                base = first // 128 * 128
                depth = min(128, lats - base)
                src = lax.broadcasted_iota(jnp.int32, (depth, size), 0)
                dst = lax.broadcasted_iota(jnp.int32, (depth, size), 1)
                spread = (src == dst // GROUP + (first - base)).astype(jnp.float32).astype(jnp.bfloat16)
                row = lax.broadcasted_iota(jnp.int32, (rows, size), 0) // ch
                col = lax.rem(lax.broadcasted_iota(jnp.int32, (rows, size), 1), GROUP)
                for side in range(2):
                    j = g * GROUP if side == 0 else m_win - GROUP - g * GROUP
                    w = wave_ref[pl.ds(pl.multiple_of(j * ch, rows), rows), base : base + depth]
                    x = jnp.dot(w, spread, preferred_element_type=jnp.float32)
                    keep = row == (col if side == 0 else GROUP - 1 - col)
                    lhs[g, side * rows : (side + 1) * rows, start : start + size] = jnp.where(
                        keep, x, 0.0
                    ).astype(jnp.bfloat16)
            return carry

        lax.fori_loop(0, half_groups, build, 0)

    slot = lax.rem(t, 2)
    col_ids = t * width + lax.broadcasted_iota(jnp.int32, (ch, width), 1)

    for step in range(half_groups):
        g = h * half_groups + step
        rhs = leg_ref[:, step * GROUP : (step + 1) * GROUP, :].reshape(lats * GROUP, width)
        both = jnp.dot(lhs[g], rhs, preferred_element_type=jnp.float32)
        for i in range(GROUP):
            p = g * GROUP + i
            low = both[i * ch : (i + 1) * ch]
            high = both[rows + (GROUP - 1 - i) * ch : rows + (GROUP - i) * ch]
            limit = length - SPACING * p - SPACING // 2
            part[slot, p] = jnp.where(col_ids < limit, low, high)

    def pair_copy(u):
        return remote(
            pair_out.at[u], pair_in.at[u], pair_send.at[u], pair_recv.at[u],
            (2 * chip + 1 - core, lev),
        )

    def chip_copy(u, d):
        return remote(
            chip_out.at[u, d - 1], chip_in.at[u, d - 1],
            chip_send.at[u, d - 1], chip_recv.at[u, d - 1],
            (2 * lax.rem(chip + d, chips) + core, lev),
        )

    def to_partner(u):
        s = lax.rem(u, 2)
        for d in range(chips):
            q = lax.rem(chip + d, chips)
            for o in range(own):
                pair_id = owner_ref[(2 * q + 1 - core) * own + o]
                pair_out[u, d * own + o] = part[s, pair_id]
        pair_copy(u).start()

    def columns(u):
        return pl.ds(pl.multiple_of(u * width, width), width)

    def to_chips(u):
        s = lax.rem(u, 2)
        pair_copy(u).wait_recv()
        for d in list(range(1, chips)) + [0]:
            q = lax.rem(chip + d, chips)
            for o in range(own):
                pair_id = owner_ref[(2 * q + core) * own + o]
                total = part[s, pair_id] + pair_in[u, d * own + o]
                if d:
                    chip_out[u, d - 1, o] = total.astype(jnp.bfloat16)
                else:
                    out_ref[o, :, columns(u)] = total
            if d:
                chip_copy(u, d).start()

    channel = lev * ch + lax.broadcasted_iota(jnp.int32, (ch, width), 0)
    factor = 1.0 + 2.0 * (channel // 2).astype(jnp.float32) / (ch * n_lev // 2 - 1)

    def collect(u):
        for d in range(1, chips):
            chip_copy(u, d).wait_recv()
        acc = jnp.zeros((ch, width), jnp.float32)
        for o in range(own):
            total = out_ref[o, :, columns(u)]
            for d in range(1, chips):
                total = total + chip_in[u, d - 1, o].astype(jnp.float32)
            out_ref[o, :, columns(u)] = total
            acc = acc + total * total
        esum[...] += acc * factor

    @pl.when((t == 0) & (h == HALVES - 1))
    def _():
        pl.semaphore_wait(barrier, n_lat - 1 + n_lev - 1)

    @pl.when((h == 0) & (t >= 1))
    def _():
        to_chips(t - 1)

    @pl.when(h == HALVES - 1)
    def _():
        to_partner(t)

    @pl.when((h == HALVES - 1) & (t >= 2))
    def _():
        collect(t - 2)

    @pl.when((h == HALVES - 1) & (t == steps - 1))
    def _():
        if steps >= 2:
            collect(steps - 2)
        to_chips(steps - 1)
        collect(steps - 1)

        def exchange(buf, send, recv, me, n, device):
            def copy(idx, d):
                return remote(
                    buf.at[idx], buf.at[idx], send.at[d - 1], recv.at[idx],
                    device(lax.rem(me + d, n)),
                )

            for d in range(1, n):
                copy(me, d).start()
            for d in range(1, n):
                copy(lax.rem(me + n - d, n), d).wait_recv()
            for d in range(1, n):
                copy(me, d).wait_send()

        acc = esum[...]
        lanes = sum(acc[:, i : i + 128] for i in range(0, width, 128))
        elat[lat] = sum(lanes[i : i + 8] for i in range(0, ch, 8))
        exchange(elat, elat_send, elat_recv, lat, n_lat, lambda i: (i, lev))
        total = elat[0]
        for i in range(1, n_lat):
            total = total + elat[i]
        elev[lev] = total
        exchange(elev, elev_send, elev_recv, lev, n_lev, lambda i: (lat, i))
        total = elev[0]
        for i in range(1, n_lev):
            total = total + elev[i]
        energy_ref[...] = jnp.full((1, 1), jnp.sum(total)) / (pairs * ch * n_lev * length)

        for u in range(steps):
            pair_copy(u).wait_send()
            for d in range(1, chips):
                chip_copy(u, d).wait_send()


def shards(n_lat, n_lev, fourier, quad_weights, legendre, owner_pair):
    weighted = (fourier.astype(jnp.float32) * quad_weights[None, :, None]).astype(jnp.bfloat16)
    ch, lats, m_win = fourier.shape
    pairs, length = legendre.shape[1:]
    width = 256
    steps = length // width
    wave = jnp.transpose(weighted, (2, 0, 1)).reshape(m_win * ch, lats)
    own = pairs // n_lat
    chips = n_lat // 2
    cfg = (n_lat, n_lev, ch, lats, pairs, length, width, steps, m_win)
    dma = pltpu.SemaphoreType.DMA
    block = pairs // HALVES
    spectra, energy = pl.pallas_call(
        functools.partial(kernel, cfg),
        grid=(steps, HALVES),
        out_shape=(
            jax.ShapeDtypeStruct((own, ch, length), jnp.float32),
            jax.ShapeDtypeStruct((1, 1), jnp.float32),
        ),
        in_specs=[
            pl.BlockSpec(memory_space=pltpu.SMEM),
            pl.BlockSpec((m_win * ch, lats), lambda t, h: (0, 0)),
            pl.BlockSpec((lats, block, width), lambda t, h: (0, h, t)),
        ],
        out_specs=(
            pl.BlockSpec((own, ch, length), lambda t, h: (0, 0, 0)),
            pl.BlockSpec((1, 1), lambda t, h: (0, 0)),
        ),
        scratch_shapes=[
            pltpu.VMEM((pairs // GROUP, 2 * GROUP * ch, lats * GROUP), jnp.bfloat16),
            pltpu.VMEM((2, pairs, ch, width), jnp.float32),
            pltpu.VMEM((steps, pairs // 2, ch, width), jnp.float32),
            pltpu.VMEM((steps, pairs // 2, ch, width), jnp.float32),
            pltpu.VMEM((steps, chips - 1, own, ch, width), jnp.bfloat16),
            pltpu.VMEM((steps, chips - 1, own, ch, width), jnp.bfloat16),
            pltpu.VMEM((ch, width), jnp.float32),
            pltpu.VMEM((n_lat, 8, 128), jnp.float32),
            pltpu.VMEM((n_lev, 8, 128), jnp.float32),
            dma((steps,)),
            dma((steps,)),
            dma((steps, chips - 1)),
            dma((steps, chips - 1)),
            dma((n_lat - 1,)),
            dma((n_lat,)),
            dma((n_lev - 1,)),
            dma((n_lev,)),
        ],
        compiler_params=pltpu.CompilerParams(
            collective_id=0,
            has_side_effects=True,
            vmem_limit_bytes=60 * 1024 * 1024,
            dimension_semantics=("arbitrary", "arbitrary"),
        ),
    )(owner_pair, wave, legendre)
    return spectra, energy.reshape(())


def solution(mesh):
    return jax.shard_map(
        functools.partial(shards, mesh.shape["lat"], mesh.shape["lev"]),
        mesh=mesh,
        in_specs=(P("lev", "lat", None), P("lat"), P("lat", None, None), P()),
        out_specs=(P("lat", "lev", None), P()),
        check_vma=False,
    )
```

profile of v0, /device:TPU:0, one launch (start us, length us, event | category | flops | bytes accessed | tf_op | source)
XLA Modules:
  0.0 54.7 jit_solution(1792838654287882621)
XLA Ops:
  0.6 1.7 %fusion = bf16[128,16,320]{0,2,1:T(8,128)(2,1)S(1)} fusion(bf16[16,320,128]{2,1,0:T(8,128)(2,1)} %param.4, f32[320]{0:T(512)} %param.5), kind=kLoop, calls=%fused_computation.1 | loop fusion | flops 1966080 | bytes 2622720 | tf_op jit(solution)/shard_map/transpose | solution.py:231
  2.4 1.9 %copy.6 = bf16[128,16,320]{2,1,0:T(8,128)(2,1)} copy(bf16[128,16,320]{0,2,1:T(8,128)(2,1)S(1)} %fusion) | data formatting | bytes 2621440 | tf_op jit(solution)/shard_map/transpose | solution.py:231
  4.3 46.7 %shard_map.59 = (f32[8,16,1280]{2,1,0:T(8,128)}, f32[1,1]{1,0:T(1,128)}) custom-call(s32[64]{0:T(128)} %owner_ref.1, bf16[2048,320]{1,0:T(8,128)(2,1)} %bitcast.4, bf16[320,64,1280]{2,1,0:T(8,128)(2,1)} %leg_ref.1), custom_call_target="tpu_custom_call" | custom-call | tf_op jit(solution)/shard_map/pallas_call | solution.py:237
  51.0 2.0 %copy.9 = f32[8,16,1280]{2,1,0:T(8,128)} copy(f32[8,16,1280]{2,1,0:T(8,128)} %get-tuple-element.8) | data formatting | bytes 1310720
where the time goes:
time: 55.1 us; the launch traced here: 54.7 us
  Pallas kernels  46.7 us (85%)
  local copies, waits for them, and re-layouts  3.9 us (7%)
  between operations  2.41 us (4%)
  other arithmetic  1.72 us (3%)
    pallas_call x1, Pallas kernels, shards(): pl.pallas_call(functools.partial(kernel, cfg), grid=(steps, HALVES), out_...  46.7 us
    unnamed x1, local copies, waits for them, and re-layouts  1.97 us
    transpose x1, local copies, waits for them, and re-layouts, shards(): wave = jnp.transpose(weighted, (2, 0, 1)).reshape(m_win * ch, lats)  1.93 us
    transpose x1, other arithmetic, shards(): wave = jnp.transpose(weighted, (2, 0, 1)).reshape(m_win * ch, lats)  1.72 us

commit v1 on v0

--- a/solution.py
+++ b/solution.py
@@ -70,8 +70,9 @@
             )
         esum[...] = jnp.zeros_like(esum)
 
-    @pl.when(t == 0)
-    def _():
+    late = int(steps > 1 and width <= length - SPACING * (pairs - 1) - SPACING // 2)
+
+    def build_side(side):
         def build(step, carry):
             g = h * half_groups + step
             for start in range(0, lats * GROUP, 256):
@@ -84,31 +85,55 @@
                 spread = (src == dst // GROUP + (first - base)).astype(jnp.float32).astype(jnp.bfloat16)
                 row = lax.broadcasted_iota(jnp.int32, (rows, size), 0) // ch
                 col = lax.rem(lax.broadcasted_iota(jnp.int32, (rows, size), 1), GROUP)
-                for side in range(2):
-                    j = g * GROUP if side == 0 else m_win - GROUP - g * GROUP
-                    w = wave_ref[pl.ds(pl.multiple_of(j * ch, rows), rows), base : base + depth]
-                    x = jnp.dot(w, spread, preferred_element_type=jnp.float32)
-                    keep = row == (col if side == 0 else GROUP - 1 - col)
-                    lhs[g, side * rows : (side + 1) * rows, start : start + size] = jnp.where(
-                        keep, x, 0.0
-                    ).astype(jnp.bfloat16)
+                j = g * GROUP if side == 0 else m_win - GROUP - g * GROUP
+                w = wave_ref[pl.ds(pl.multiple_of(j * ch, rows), rows), base : base + depth]
+                x = jnp.dot(w, spread, preferred_element_type=jnp.float32)
+                keep = row == (col if side == 0 else GROUP - 1 - col)
+                lhs[g, side * rows : (side + 1) * rows, start : start + size] = jnp.where(
+                    keep, x, 0.0
+                ).astype(jnp.bfloat16)
             return carry
 
         lax.fori_loop(0, half_groups, build, 0)
+
+    @pl.when(t == 0)
+    def _():
+        build_side(0)
+
+    @pl.when(t == late)
+    def _():
+        build_side(1)
 
     slot = lax.rem(t, 2)
     col_ids = t * width + lax.broadcasted_iota(jnp.int32, (ch, width), 1)
 
     for step in range(half_groups):
         g = h * half_groups + step
-        rhs = leg_ref[:, step * GROUP : (step + 1) * GROUP, :].reshape(lats * GROUP, width)
-        both = jnp.dot(lhs[g], rhs, preferred_element_type=jnp.float32)
-        for i in range(GROUP):
-            p = g * GROUP + i
-            low = both[i * ch : (i + 1) * ch]
-            high = both[rows + (GROUP - 1 - i) * ch : rows + (GROUP - i) * ch]
-            limit = length - SPACING * p - SPACING // 2
-            part[slot, p] = jnp.where(col_ids < limit, low, high)
+        span = slice(step * GROUP, (step + 1) * GROUP)
+        top = length - SPACING * GROUP * g - SPACING // 2
+        is_low = (t + 1) * width <= top - SPACING * (GROUP - 1)
+        is_high = t * width >= top
+
+        @pl.when(is_low | is_high)
+        def _():
+            side = is_high.astype(jnp.int32)
+            rhs = leg_ref[:, span, :].reshape(lats * GROUP, width)
+            left = lhs[g, pl.ds(pl.multiple_of(side * rows, rows), rows), :]
+            one = jnp.dot(left, rhs, preferred_element_type=jnp.float32)
+            for i in range(GROUP):
+                p = g * GROUP + i + side * (GROUP - 1 - 2 * i)
+                part[slot, p] = one[i * ch : (i + 1) * ch]
+
+        @pl.when(jnp.logical_not(is_low | is_high))
+        def _():
+            rhs = leg_ref[:, span, :].reshape(lats * GROUP, width)
+            both = jnp.dot(lhs[g], rhs, preferred_element_type=jnp.float32)
+            for i in range(GROUP):
+                p = g * GROUP + i
+                low = both[i * ch : (i + 1) * ch]
+                high = both[rows + (GROUP - 1 - i) * ch : rows + (GROUP - i) * ch]
+                limit = length - SPACING * p - SPACING // 2
+                part[slot, p] = jnp.where(col_ids < limit, low, high)
 
     def pair_copy(u):
         return remote(

time: 55.1 us -> 55.8 us (1.013)
  Pallas kernels: 46.7 us -> 47.4 us
    pallas_call x1, Pallas kernels: 46.7 us -> 47.4 us  [shards(): pl.pallas_call(functools.partial(kernel, cfg), grid=(steps, HALVES), out_...]
where the time goes in v1:
time: 55.8 us; the launch traced here: 55.5 us
  Pallas kernels  47.4 us (85%)
  local copies, waits for them, and re-layouts  3.9 us (7%)
  between operations  2.41 us (4%)
  other arithmetic  1.72 us (3%)
    pallas_call x1, Pallas kernels, shards(): pl.pallas_call(functools.partial(kernel, cfg), grid=(steps, HALVES), out_...  47.4 us
    unnamed x1, local copies, waits for them, and re-layouts  1.97 us
    transpose x1, local copies, waits for them, and re-layouts, shards(): wave = jnp.transpose(weighted, (2, 0, 1)).reshape(m_win * ch, lats)  1.93 us
    transpose x1, other arithmetic, shards(): wave = jnp.transpose(weighted, (2, 0, 1)).reshape(m_win * ch, lats)  1.72 us

profile of v1, /device:TPU:0, one launch (start us, length us, event | category | flops | bytes accessed | tf_op | source)
XLA Modules:
  0.0 55.5 jit_solution(9379341338208903392)
XLA Ops:
  0.6 1.7 %fusion = bf16[128,16,320]{0,2,1:T(8,128)(2,1)S(1)} fusion(bf16[16,320,128]{2,1,0:T(8,128)(2,1)} %param.4, f32[320]{0:T(512)} %param.5), kind=kLoop, calls=%fused_computation.1 | loop fusion | flops 1966080 | bytes 2622720 | tf_op jit(solution)/shard_map/transpose | solution.py:256
  2.4 1.9 %copy.6 = bf16[128,16,320]{2,1,0:T(8,128)(2,1)} copy(bf16[128,16,320]{0,2,1:T(8,128)(2,1)S(1)} %fusion) | data formatting | bytes 2621440 | tf_op jit(solution)/shard_map/transpose | solution.py:256
  4.3 47.4 %shard_map.59 = (f32[8,16,1280]{2,1,0:T(8,128)}, f32[1,1]{1,0:T(1,128)}) custom-call(s32[64]{0:T(128)} %owner_ref.1, bf16[2048,320]{1,0:T(8,128)(2,1)} %bitcast.4, bf16[320,64,1280]{2,1,0:T(8,128)(2,1)} %leg_ref.1), custom_call_target="tpu_custom_call" | custom-call | tf_op jit(solution)/shard_map/pallas_call | solution.py:262
  51.7 2.0 %copy.9 = f32[8,16,1280]{2,1,0:T(8,128)} copy(f32[8,16,1280]{2,1,0:T(8,128)} %get-tuple-element.8) | data formatting | bytes 1310720
